TPU v7x, 32 devices: a whole 2x2x4 slice. The times are simulated.
32 devices in a mesh: row: 8 (over z, x), col: 4 (over y, core).
Axes of the slice: x: 2, y: 2, z: 4, core: 2. Of those that a mesh axis runs over, the one named last changes fastest.
Arguments:
- offsets: int32 [8, 4, 2], P('row', 'col'), may hold values from 1 to 3
- targets: float32 [3, 3, 256, 512], P(None, None, 'row', 'col'), may hold values from -60 to 60
- grid_fine: float32 [32, 256, 512], P(None, 'row', 'col'), may hold values from -6 to 6
- grid_coarse: float32 [32, 64, 128], P(None, 'row', 'col'), may hold values from -6 to 6
- weight_in: float32 [512, 64], replicated, may hold values from -0.75 to 0.75
- weight_mid: float32 [1, 512, 512], replicated, may hold values from -0.25 to 0.25
- weight_out: float32 [3, 512], replicated, may hold values from -0.397747564 to 0.397747564
- fine_first: float32 [32, 256, 512], P(None, 'row', 'col'), may hold values from -0.012 to 0.012
- fine_second: float32 [32, 256, 512], P(None, 'row', 'col'), may hold values from 1e-06 to 0.0001
- coarse_first: float32 [32, 64, 128], P(None, 'row', 'col'), may hold values from -0.012 to 0.012
- coarse_second: float32 [32, 64, 128], P(None, 'row', 'col'), may hold values from 1e-06 to 0.0001
- in_first: float32 [512, 64], replicated, may hold values from -0.012 to 0.012
- in_second: float32 [512, 64], replicated, may hold values from 1e-06 to 0.0001
- mid_first: float32 [1, 512, 512], replicated, may hold values from -0.012 to 0.012
- mid_second: float32 [1, 512, 512], replicated, may hold values from 1e-06 to 0.0001
- out_first: float32 [3, 512], replicated, may hold values from -0.012 to 0.012
- out_second: float32 [3, 512], replicated, may hold values from 1e-06 to 0.0001
Outputs:
- fine_step: float32 [32, 256, 512], P(None, 'row', 'col')
- coarse_step: float32 [32, 64, 128], P(None, 'row', 'col')
- input_step: float32 [512, 64], replicated
- middle_step: float32 [1, 512, 512], replicated
- output_step: float32 [3, 512], replicated
All inputs are finite; a program needn't handle non-finite values.
Results may differ from a plain program's by a relative error of at most 0.0014.
The roundings to bfloat16 on the way count: a program that leaves them out, or rounds other values in their place, can miss the bound.
Values sent between devices are 32-bit elements; how exact they have to be, the bound alone decides.
A program may use at most 64 MiB of HBM per device.

v0:
```python
import jax
import jax.numpy as jnp
from jax import lax
from jax.sharding import PartitionSpec as P

SUB = 4
RATIO = 4
ADAM_STEP = 10
BETA_ONE = 0.9
BETA_TWO = 0.99
ADAM_EPSILON = 1e-08
CLIP_RMS = 0.01
LOSS_VALUE = 0.25
MEAN_EPSILON = 1e-06


def shifted(block, axis, distance):
    devices = range(lax.axis_size(axis))
    route = [(i - distance, i) for i in devices if i - distance in devices]
    return lax.ppermute(block, axis, route)


def interp_table(samples, level_ratio, offset):
    positions = jnp.arange(samples, dtype=jnp.int32)
    base_index = positions // level_ratio
    fraction = (
        (positions % level_ratio).astype(jnp.float32) + offset.astype(jnp.float32) / SUB
    ) / level_ratio
    column = jnp.arange(samples // level_ratio + 1, dtype=jnp.int32)
    lower_hit = (column[None, :] == base_index[:, None]).astype(jnp.float32)
    upper_hit = (column[None, :] == base_index[:, None] + 1).astype(jnp.float32)
    return lower_hit * (1.0 - fraction)[:, None] + upper_hit * fraction[:, None]


def level_tables(row_count, col_count, shift_y, shift_x):
    return (
        interp_table(row_count, 1, shift_y),
        interp_table(col_count, 1, shift_x),
        interp_table(row_count, RATIO, shift_y),
        interp_table(col_count, RATIO, shift_x),
    )


def sample_level(extended, row_table, col_table):
    across = jnp.einsum("kjl,ml->kjm", extended, col_table, precision=lax.Precision.HIGHEST)
    return jnp.einsum("ij,kjm->kim", row_table, across, precision=lax.Precision.HIGHEST)


def spread_level(cotangent, row_table, col_table):
    backward = jnp.einsum("ij,kim->kjm", row_table, cotangent, precision=lax.Precision.HIGHEST)
    return jnp.einsum("kjm,ml->kjl", backward, col_table, precision=lax.Precision.HIGHEST)


def sample_features(fine_ext, coarse_ext, tables):
    fine_feat = sample_level(fine_ext, tables[0], tables[1])
    coarse_feat = sample_level(coarse_ext, tables[2], tables[3])
    channels, row_count, col_count = fine_feat.shape
    return jnp.concatenate(
        [
            fine_feat.reshape(channels, row_count * col_count),
            coarse_feat.reshape(channels, row_count * col_count),
        ],
        axis=0,
    ).astype(jnp.bfloat16)


def spread_features(feature_grad, tables):
    channels = feature_grad.shape[0] // 2
    row_count = tables[0].shape[0]
    col_count = tables[1].shape[0]
    fine_cot = feature_grad[:channels].reshape(channels, row_count, col_count)
    coarse_cot = feature_grad[channels:].reshape(channels, row_count, col_count)
    return (
        spread_level(fine_cot, tables[0], tables[1]),
        spread_level(coarse_cot, tables[2], tables[3]),
    )


def matmul(former, latter):
    return jnp.dot(former, latter, preferred_element_type=jnp.float32)


def contract_rows(former, latter):
    return lax.dot_general(
        former, latter, (((0,), (0,)), ((), ())), preferred_element_type=jnp.float32
    )


def contract_cols(former, latter):
    return lax.dot_general(
        former, latter, (((1,), (1,)), ((), ())), preferred_element_type=jnp.float32
    )


def silu_slope(pre_act):
    sigmoid = jax.nn.sigmoid(pre_act)
    return sigmoid * (1.0 + pre_act * (1.0 - sigmoid))


def decoder_forward(features, low_in, low_mid, low_out):
    pre_acts = [matmul(low_in, features)]
    activations = [jax.nn.silu(pre_acts[0]).astype(jnp.bfloat16)]
    pre_acts.append(matmul(low_mid[0], activations[-1]))
    activations.append(jax.nn.silu(pre_acts[-1]).astype(jnp.bfloat16))
    return (matmul(low_out, activations[-1]), pre_acts, activations)


def decoder_backward(features, pre_acts, activations, cotangent, low_in, low_mid, low_out):
    out_cotangent = cotangent.astype(jnp.bfloat16)
    grad_out = contract_cols(out_cotangent, activations[-1])
    upward = contract_rows(low_out, out_cotangent)
    grads_mid = []
    delta_low = (upward * silu_slope(pre_acts[1])).astype(jnp.bfloat16)
    grads_mid.insert(0, contract_cols(delta_low, activations[0]))
    upward = contract_rows(low_mid[0], delta_low)
    delta_low = (upward * silu_slope(pre_acts[0])).astype(jnp.bfloat16)
    grad_in = contract_cols(delta_low, features)
    feature_grad = contract_rows(low_in, delta_low)
    return (grad_in, jnp.stack(grads_mid), grad_out, feature_grad)


def pixel_cotangent(value_error, row_error, row_prior, col_error, col_prior):
    return (
        2.0 * LOSS_VALUE * value_error
        + 2.0 * (row_prior - row_error)
        + 2.0 * (col_prior - col_error)
    )


def clip_factor(total, entries):
    return jnp.minimum(1.0, CLIP_RMS / jnp.sqrt(total / entries + MEAN_EPSILON))


def adam_step(gradient, moment_one, moment_two, clip_scale):
    clipped = gradient * clip_scale
    new_one = BETA_ONE * moment_one + (1.0 - BETA_ONE) * clipped
    new_two = BETA_TWO * moment_two + (1.0 - BETA_TWO) * clipped * clipped
    return (
        new_one
        / (1.0 - BETA_ONE**ADAM_STEP)
        / (jnp.sqrt(new_two / (1.0 - BETA_TWO**ADAM_STEP)) + ADAM_EPSILON)
    )


def grid_total_sum(grid_local):
    return lax.psum(grid_local, ("row", "col"))


def shards(
    offsets,
    targets,
    grid_fine,
    grid_coarse,
    weight_in,
    weight_mid,
    weight_out,
    fine_first,
    fine_second,
    coarse_first,
    coarse_second,
    in_first,
    in_second,
    mid_first,
    mid_second,
    out_first,
    out_second,
):
    channels, sample_rows, sample_cols = grid_fine.shape
    coarse_rows = grid_coarse.shape[1]
    coarse_cols = grid_coarse.shape[2]
    low_in = weight_in.astype(jnp.bfloat16)
    low_mid = weight_mid.astype(jnp.bfloat16)
    low_out = weight_out.astype(jnp.bfloat16)
    top_rows = jnp.concatenate([grid_fine[:, :1, :], grid_coarse[:, :1, :]], axis=2)
    top_rows = shifted(top_rows, "row", -1)
    fine_tall = jnp.concatenate([grid_fine, top_rows[:, :, :sample_cols]], axis=1)
    coarse_tall = jnp.concatenate([grid_coarse, top_rows[:, :, sample_cols:]], axis=1)
    edge_cols = jnp.concatenate([fine_tall[:, :, :1], coarse_tall[:, :, :1]], axis=1)
    edge_cols = shifted(edge_cols, "col", -1)
    fine_ext = jnp.concatenate([fine_tall, edge_cols[:, : sample_rows + 1, :]], axis=2)
    coarse_ext = jnp.concatenate([coarse_tall, edge_cols[:, sample_rows + 1 :, :]], axis=2)
    tables = level_tables(sample_rows, sample_cols, offsets[0, 0, 0], offsets[0, 0, 1])
    features = sample_features(fine_ext, coarse_ext, tables)
    predicted, pre_acts, activations = decoder_forward(features, low_in, low_mid, low_out)
    outputs = predicted.shape[0]
    predicted = predicted.reshape(outputs, sample_rows, sample_cols)
    below = shifted(predicted[:, :1, :], "row", -1)
    beside = shifted(predicted[:, :, :1], "col", -1)
    row_global = lax.axis_index("row") * sample_rows + jnp.arange(sample_rows, dtype=jnp.int32)
    col_global = lax.axis_index("col") * sample_cols + jnp.arange(sample_cols, dtype=jnp.int32)
    row_valid = (row_global < lax.axis_size("row") * sample_rows - 1)[None, :, None]
    col_valid = (col_global < lax.axis_size("col") * sample_cols - 1)[None, None, :]
    row_next = jnp.concatenate([predicted[:, 1:, :], below], axis=1)
    col_next = jnp.concatenate([predicted[:, :, 1:], beside], axis=2)
    value_error = predicted - targets[0]
    row_error = jnp.where(row_valid, row_next - predicted - targets[1], 0.0)
    col_error = jnp.where(col_valid, col_next - predicted - targets[2], 0.0)
    above = shifted(row_error[:, -1:, :], "row", 1)
    before = shifted(col_error[:, :, -1:], "col", 1)
    row_prior = jnp.concatenate([above, row_error[:, :-1, :]], axis=1)
    col_prior = jnp.concatenate([before, col_error[:, :, :-1]], axis=2)
    cotangent = pixel_cotangent(value_error, row_error, row_prior, col_error, col_prior)
    grad_in, grad_mid, grad_out, feature_grad = decoder_backward(
        features,
        pre_acts,
        activations,
        cotangent.reshape(outputs, sample_rows * sample_cols),
        low_in,
        low_mid,
        low_out,
    )
    fine_back, coarse_back = spread_features(feature_grad, tables)
    side_cols = jnp.concatenate(
        [fine_back[:, :, sample_cols:], coarse_back[:, :, coarse_cols:]], axis=1
    )
    side_cols = shifted(side_cols, "col", 1)
    fine_tall_grad = jnp.concatenate(
        [fine_back[:, :, :1] + side_cols[:, : sample_rows + 1, :], fine_back[:, :, 1:sample_cols]],
        axis=2,
    )
    coarse_tall_grad = jnp.concatenate(
        [
            coarse_back[:, :, :1] + side_cols[:, sample_rows + 1 :, :],
            coarse_back[:, :, 1:coarse_cols],
        ],
        axis=2,
    )
    bottom_rows = jnp.concatenate(
        [fine_tall_grad[:, sample_rows:, :], coarse_tall_grad[:, coarse_rows:, :]], axis=2
    )
    bottom_rows = shifted(bottom_rows, "row", 1)
    fine_grad = jnp.concatenate(
        [
            fine_tall_grad[:, :1, :] + bottom_rows[:, :, :sample_cols],
            fine_tall_grad[:, 1:sample_rows, :],
        ],
        axis=1,
    )
    coarse_grad = jnp.concatenate(
        [
            coarse_tall_grad[:, :1, :] + bottom_rows[:, :, sample_cols:],
            coarse_tall_grad[:, 1:coarse_rows, :],
        ],
        axis=1,
    )
    grid_local = jnp.sum(fine_grad * fine_grad) + jnp.sum(coarse_grad * coarse_grad)
    devices = lax.axis_size("row") * lax.axis_size("col")
    grid_entries = (fine_grad.size + coarse_grad.size) * devices
    decoder_entries = weight_in.size + weight_mid.size + weight_out.size
    grad_in, grad_mid, grad_out = lax.psum((grad_in, grad_mid, grad_out), ("row", "col"))
    grid_total = grid_total_sum(grid_local)
    decoder_total = (
        jnp.sum(grad_in * grad_in) + jnp.sum(grad_mid * grad_mid) + jnp.sum(grad_out * grad_out)
    )
    decoder_scale = clip_factor(decoder_total, decoder_entries)
    middle_step = adam_step(grad_mid, mid_first, mid_second, decoder_scale)
    grid_scale = clip_factor(grid_total, grid_entries)
    fine_step = adam_step(fine_grad, fine_first, fine_second, grid_scale)
    coarse_step = adam_step(coarse_grad, coarse_first, coarse_second, grid_scale)
    input_step = adam_step(grad_in, in_first, in_second, decoder_scale)
    output_step = adam_step(grad_out, out_first, out_second, decoder_scale)
    return (fine_step, coarse_step, input_step, middle_step, output_step)


def solution(mesh):
    placed = (
        P("row", "col", None),
        P(None, None, "row", "col"),
        P(None, "row", "col"),
        P(None, "row", "col"),
        P(),
        P(),
        P(),
        P(None, "row", "col"),
        P(None, "row", "col"),
        P(None, "row", "col"),
        P(None, "row", "col"),
        P(),
        P(),
        P(),
        P(),
        P(),
        P(),
    )
    return jax.shard_map(
        shards,
        mesh=mesh,
        in_specs=placed,
        out_specs=(P(None, "row", "col"), P(None, "row", "col"), P(), P(), P()),
        check_vma=False,
    )
```

profile of v0, /device:TPU:0, one launch (start us, length us, event | category | flops | bytes accessed | tf_op | source)
XLA Modules:
  0.0 238.9 jit_solution(828096831755790455)
XLA Ops:
  7.2 0.9 slice.117
  8.2 0.9 copy.59
  9.2 1.3 collective-permute-start
  10.5 1.3 fusion.148
  13.1 0.9 slice_bitcast_fusion.2
  14.0 1.9 collective-permute-done
  16.3 1.1 pad_maximum_fusion
  17.8 1.3 collective-permute-start.1
  19.1 1.8 collective-permute-done.1
  21.6 2.2 fusion.14
  23.8 0.6 convolution_convert_fusion.1
  24.9 0.6 convolution_convert_fusion
  25.6 1.3 fusion.82
  26.9 4.4 %fusion.5 = (bf16[512,4096]{0,1:T(8,128)(2,1)S(1)}, f32[4096,512]{1,0:T(8,128)S(1)}) fusion(f32[1,512,512]{2,1,0:T(8,128)S(1)} %copy-done.11, f32[4096,512]{1,0:T(8,128)S(1)} %fusion.82), kind=kOutput, calls=%fused_computation.10 | convolution fusion | flops 2168717312 | bytes 22020096 | tf_op jit(solution)/shard_map/dot_general | solution.py:80
  31.4 1.2 fusion.125
  32.6 1.3 collective-permute-start.2
  33.9 1.3 collective-permute-start.4
  35.3 3.6 %collective-permute-done.4 = f32[3,32,1]{2,1,0:T(8,128)S(1)} collective-permute-done((f32[3,32,1]{2,1,0:T(8,128)S(1)}, f32[3,32,1]{2,1,0:T(8,128)S(1)}, u32[]{:S(2)}, u32[]{:S(2)}) %collective-permute-start.4) | collective-permute-done | bytes 416 | tf_op jit(solution)/shard_map/ppermute | solution.py:20
  39.1 4.6 %collective-permute-start.5 = (f32[3,32,1]{2,1,0:T(8,128)S(1)}, f32[3,32,1]{2,1,0:T(8,128)S(1)}, u32[]{:S(2)}, u32[]{:S(2)}) collective-permute-start(f32[3,32,1]{2,1,0:T(8,128)S(1)} %slice.167), channel_id=1, source_target_pairs={{0,1},{1,2},{2,3},{4,5},{5,6},{6,7},{8,9},{9,10},{10,11},{12,13},{... | collective-permute-start | bytes 1160 | tf_op jit(solution)/shard_map/ppermute | solution.py:20
  43.8 5.1 %collective-permute-start.3 = (f32[3,1,128]{2,1,0:T(1,128)S(1)}, f32[3,1,128]{2,1,0:T(1,128)S(1)}, u32[]{:S(2)}, u32[]{:S(2)}) collective-permute-start(f32[3,1,128]{2,1,0:T(1,128)S(1)} %slice.163), channel_id=1, source_target_pairs={{0,4},{4,8},{8,12},{12,16},{16,20},{20,24},{24,28},{1,5},{5,9},{9,... | collective-permute-start | bytes 4616 | tf_op jit(solution)/shard_map/ppermute | solution.py:20
  49.0 1.0 collective-permute-done.3
  50.3 3.5 %fusion.1 = bf16[512,4096]{0,1:T(8,128)(2,1)S(1)} fusion(f32[4096,512]{1,0:T(8,128)S(1)} %get-tuple-element.27, bf16[3,4096]{1,0:T(4,128)(2,1)S(1)} %fusion.63, f32[3,512]{1,0:T(4,128)S(1)} %copy-done.8), kind=kOutput, calls=%fused_computation.3 | convolution fusion | flops 31458816 | bytes 12613632 | tf_op jit(solution)/shard_map/dot_general | solution.py:84
  53.8 3.4 %convolution_bitcast_fusion.1 = f32[1,512,512]{2,1,0:T(8,128)} fusion(bf16[512,4096]{0,1:T(8,128)(2,1)S(1)} %fusion.1, f32[4096,512]{1,0:T(8,128)S(1)} %fusion.82), kind=kOutput, calls=%fused_computation.24 | convolution fusion | flops 2157969408 | bytes 13631488 | tf_op jit(solution)/shard_map/dot_general | solution.py:90
  57.3 3.6 %fusion = bf16[512,4096]{0,1:T(8,128)(2,1)S(1)} fusion(f32[4096,512]{1,0:T(8,128)S(1)} %fusion.82, bf16[512,4096]{0,1:T(8,128)(2,1)S(1)} %fusion.1, f32[1,512,512]{2,1,0:T(8,128)S(1)} %copy-done.11), kind=kOutput, calls=%fused_computation.1 | convolution fusion | flops 2166620160 | bytes 17825792 | tf_op jit(solution)/shard_map/dot_general | solution.py:84
  60.9 2.0 copy-done.1
  62.8 1.4 convolution_bitcast_fusion
  64.4 0.4 convolution_bitcast_fusion.3
  65.1 0.7 fusion.147
  66.2 0.8 convolution_bitcast_fusion.2
  67.0 1.2 fusion.56
  68.7 1.3 collective-permute-start.6
  70.0 3.7 %fusion.150 = f32[512,64]{0,1:T(8,128)} fusion(bf16[64,4096]{1,0:T(8,128)(2,1)S(1)} %bitcast_dynamic-update-slice_fusion, bf16[512,4096]{0,1:T(8,128)(2,1)} %copy-done.1), kind=kOutput, calls=%fused_computation.235 | convolution fusion | flops 268435456 | bytes 4849664 | tf_op jit(solution)/shard_map/dot_general | solution.py:90
  74.1 1.2 copy.74
  76.0 0.4 copy.72
  76.6 4.9 %collective-permute-start.7 = (f32[32,1,160]{2,1,0:T(1,128)S(1)}, f32[32,1,160]{2,1,0:T(1,128)S(1)}, u32[]{:S(2)}, u32[]{:S(2)}) collective-permute-start(f32[32,1,160]{2,1,0:T(1,128)S(1)} %fusion.80), channel_id=1, source_target_pairs={{0,4},{4,8},{8,12},{12,16},{16,20},{20,24},{24,28},{1,5},{5,9},{9,... | collective-permute-start | bytes 61448 | tf_op jit(solution)/shard_map/ppermute | solution.py:20
  81.5 2.8 %fusion.149 = f32[3,512]{1,0:T(4,128)S(1)} fusion(bf16[3,4096]{1,0:T(4,128)(2,1)S(1)} %fusion.63, bf16[512,4096]{0,1:T(8,128)(2,1)} %copy-done), kind=kOutput, calls=%fused_computation.234 | convolution fusion | flops 12582912 | bytes 4225024 | tf_op jit(solution)/shard_map/dot_general | solution.py:90
  84.4 0.8 multiply_reduce_fusion.1
  85.3 0.7 multiply_reduce_fusion.3
  87.4 41.9 %all-reduce = (f32[]{:T(128)}, f32[3,512]{1,0:T(4,128)S(1)}) all-reduce(f32[]{:T(128)S(6)} %add.300, f32[3,512]{1,0:T(4,128)S(1)} %fusion.149), channel_id=1, replica_groups=mesh['row'=8,'col'=4] {'row','col'}, use_global_device_ids=true, to_apply=%region_2.3 | all-reduce | flops 1537 | bytes 12296 | tf_op jit(solution)/shard_map/psum | solution.py:146
  129.9 0.7 multiply_reduce_fusion.4
  130.6 1.7 fusion.49
  132.3 2.5 %fusion.29 = f32[32,32,128]{2,1,0:T(8,128)} fusion(f32[32,32,128]{2,1,0:T(8,128)} %param.25, f32[32,32,128]{2,1,0:T(8,128)} %param.24, f32[]{:T(128)S(6)} %min.6, f32[32,33,127]{2,1,0:T(8,128)S(1)} %slice.175, f32[32,33,1]{2,1,0:T(8,128)S(1)} %copy.72, f32[32,1,128]{2,1,0:T(1,128)S(1)} %slice_add_fusion.1), kind=kLoop, calls=%fused_computation.47 | loop fusion | flops 2228224 | bytes 2129924 | tf_op jit(solution)/shard_map/div | solution.py:139
  134.7 86.2 %all-reduce.4.cloned.1.call-done = (f32[512,64]{0,1:T(8,128)}, f32[1,512,512]{2,1,0:T(8,128)}) async-done(((f32[512,64]{0,1:T(8,128)}, f32[1,512,512]{2,1,0:T(8,128)}), (f32[512,64]{0,1:T(8,128)}, f32[1,512,512]{2,1,0:T(8,128)})) %all-reduce.4.cloned.1.call-update) | async-done | bytes 1179664 | tf_op jit(solution)/shard_map/psum | solution.py:250
  220.9 2.1 multiply_reduce_fusion
  223.0 1.5 multiply_reduce_fusion.2
  226.6 0.6 fusion.103
  227.2 3.2 %fusion.24 = f32[1,512,512]{2,1,0:T(8,128)} fusion(f32[1,512,512]{2,1,0:T(8,128)S(1)} %copy-done.2, f32[1,512,512]{2,1,0:T(8,128)} %get-tuple-element.8, f32[1,512,512]{2,1,0:T(8,128)} %param.30, f32[]{:T(128)S(6)} %min.7), kind=kLoop, calls=%fused_computation.39 | loop fusion | flops 3145728 | bytes 4194308 | tf_op jit(solution)/shard_map/div | solution.py:139
  230.4 1.7 fusion.54
  (81 shorter events, 5.7 us)
Async XLA Ops:
  7.2 18.5 %copy-start.3 = (f32[512,64]{0,1:T(8,128)S(1)}, f32[512,64]{0,1:T(8,128)}, u32[]{:S(2)}) copy-start(f32[512,64]{0,1:T(8,128)} %param.21) | copy-start | bytes 393220
  7.2 213.8 %all-reduce.4.cloned.1.call-start = ((), (), s32[]{:S(2)}) async-start(), calls=%async_computation | async-start | bytes 2359296 | tf_op jit(solution)/shard_map/psum | solution.py:250
  9.2 6.8 %collective-permute-start = (f32[32,1,160]{2,1,0:T(1,128)S(1)}, f32[32,1,160]{2,1,0:T(1,128)S(1)}, u32[]{:S(2)}, u32[]{:S(2)}) collective-permute-start(f32[32,1,160]{2,1,0:T(1,128)S(1)} %copy.60), channel_id=1, source_target_pairs={{4,0},{8,4},{12,8},{16,12},{20,16},{24,20},{28,24},{5,1},{9,5},{13... | collective-permute-start | bytes 61448 | tf_op jit(solution)/shard_map/ppermute | solution.py:20
  17.8 3.1 %collective-permute-start.1 = (f32[32,42,1]{1,0,2:T(8,128)S(1)}, f32[32,42,1]{1,0,2:T(8,128)S(1)}, u32[]{:S(2)}, u32[]{:S(2)}) collective-permute-start(f32[32,42,1]{1,0,2:T(8,128)S(1)} %pad_maximum_fusion.7), channel_id=1, source_target_pairs={{1,0},{2,1},{3,2},{5,4},{6,5},{7,6},{9,8},{10,9},{11,10},{13,12},{... | collective-permute-start | bytes 16136 | tf_op jit(solution)/shard_map/ppermute | solution.py:20
  23.8 3.1 %copy-start.11 = (f32[1,512,512]{2,1,0:T(8,128)S(1)}, f32[1,512,512]{2,1,0:T(8,128)}, u32[]{:S(2)}) copy-start(f32[1,512,512]{2,1,0:T(8,128)} %param.22) | copy-start | bytes 3145732
  26.9 4.4 %copy-start.8 = (f32[3,512]{1,0:T(4,128)S(1)}, f32[3,512]{1,0:T(4,128)}, u32[]{:S(2)}) copy-start(f32[3,512]{1,0:T(4,128)} %param.23) | copy-start | bytes 18436
  26.9 12.0 %copy-start.4 = (f32[3,3,32,128]{3,2,1,0:T(8,128)S(1)}, f32[3,3,32,128]{3,2,1,0:T(8,128)}, u32[]{:S(2)}) copy-start(f32[3,3,32,128]{3,2,1,0:T(8,128)} %param.18) | copy-start | bytes 442372
  31.4 22.5 %copy-start = (bf16[512,4096]{0,1:T(8,128)(2,1)}, bf16[512,4096]{0,1:T(8,128)(2,1)S(1)}, u32[]{:S(2)}) copy-start(bf16[512,4096]{0,1:T(8,128)(2,1)S(1)} %get-tuple-element.26) | copy-start | bytes 12582916
  32.6 6.4 %collective-permute-start.2 = (f32[3,1,128]{2,1,0:T(1,128)S(1)}, f32[3,1,128]{2,1,0:T(1,128)S(1)}, u32[]{:S(2)}, u32[]{:S(2)}) collective-permute-start(f32[3,1,128]{2,1,0:T(1,128)S(1)} %slice.162), channel_id=1, source_target_pairs={{4,0},{8,4},{12,8},{16,12},{20,16},{24,20},{28,24},{5,1},{9,5},{13... | collective-permute-start | bytes 4616 | tf_op jit(solution)/shard_map/ppermute | solution.py:20
  33.9 5.0 %collective-permute-start.4 = (f32[3,32,1]{2,1,0:T(8,128)S(1)}, f32[3,32,1]{2,1,0:T(8,128)S(1)}, u32[]{:S(2)}, u32[]{:S(2)}) collective-permute-start(f32[3,32,1]{2,1,0:T(8,128)S(1)} %bitcast.213), channel_id=1, source_target_pairs={{1,0},{2,1},{3,2},{5,4},{6,5},{7,6},{9,8},{10,9},{11,10},{13,12},{... | collective-permute-start | bytes 1160 | tf_op jit(solution)/shard_map/ppermute | solution.py:20
  39.1 9.8 %collective-permute-start.5 = (f32[3,32,1]{2,1,0:T(8,128)S(1)}, f32[3,32,1]{2,1,0:T(8,128)S(1)}, u32[]{:S(2)}, u32[]{:S(2)}) collective-permute-start(f32[3,32,1]{2,1,0:T(8,128)S(1)} %slice.167), channel_id=1, source_target_pairs={{0,1},{1,2},{2,3},{4,5},{5,6},{6,7},{8,9},{9,10},{10,11},{12,13},{... | collective-permute-start | bytes 1160 | tf_op jit(solution)/shard_map/ppermute | solution.py:20
  43.8 6.2 %collective-permute-start.3 = (f32[3,1,128]{2,1,0:T(1,128)S(1)}, f32[3,1,128]{2,1,0:T(1,128)S(1)}, u32[]{:S(2)}, u32[]{:S(2)}) collective-permute-start(f32[3,1,128]{2,1,0:T(1,128)S(1)} %slice.163), channel_id=1, source_target_pairs={{0,4},{4,8},{8,12},{12,16},{16,20},{20,24},{24,28},{1,5},{5,9},{9,... | collective-permute-start | bytes 4616 | tf_op jit(solution)/shard_map/ppermute | solution.py:20
  60.8 2.0 copy-start.1
  68.7 6.9 %collective-permute-start.6 = (f32[32,42,1]{1,0,2:T(8,128)S(1)}, f32[32,42,1]{1,0,2:T(8,128)S(1)}, u32[]{:S(2)}, u32[]{:S(2)}) collective-permute-start(f32[32,42,1]{1,0,2:T(8,128)S(1)} %pad_maximum_fusion.8), channel_id=1, source_target_pairs={{0,1},{1,2},{2,3},{4,5},{5,6},{6,7},{8,9},{9,10},{10,11},{12,13},{... | collective-permute-start | bytes 16136 | tf_op jit(solution)/shard_map/ppermute | solution.py:20
  73.6 57.0 %copy-start.5 = (f32[32,8,32]{2,1,0:T(8,128)S(1)}, f32[32,8,32]{2,1,0:T(8,128)}, u32[]{:S(2)}) copy-start(f32[32,8,32]{2,1,0:T(8,128)} %param.27) | copy-start | bytes 98308
  75.7 150.9 %copy-start.9 = (f32[3,512]{1,0:T(4,128)S(1)}, f32[3,512]{1,0:T(4,128)}, u32[]{:S(2)}) copy-start(f32[3,512]{1,0:T(4,128)} %param.33) | copy-start | bytes 18436
  75.7 150.9 %copy-start.10 = (f32[3,512]{1,0:T(4,128)S(1)}, f32[3,512]{1,0:T(4,128)}, u32[]{:S(2)}) copy-start(f32[3,512]{1,0:T(4,128)} %param.32) | copy-start | bytes 18436
  75.7 151.5 %copy-start.2 = (f32[1,512,512]{2,1,0:T(8,128)S(1)}, f32[1,512,512]{2,1,0:T(8,128)}, u32[]{:S(2)}) copy-start(f32[1,512,512]{2,1,0:T(8,128)} %param.31) | copy-start | bytes 3145732
  76.5 153.9 %copy-start.6 = (f32[512,64]{0,1:T(8,128)S(1)}, f32[512,64]{0,1:T(8,128)}, u32[]{:S(2)}) copy-start(f32[512,64]{0,1:T(8,128)} %param.29) | copy-start | bytes 393220
  76.5 153.8 %copy-start.7 = (f32[512,64]{0,1:T(8,128)S(1)}, f32[512,64]{0,1:T(8,128)}, u32[]{:S(2)}) copy-start(f32[512,64]{0,1:T(8,128)} %param.28) | copy-start | bytes 393220
  76.6 7.7 %collective-permute-start.7 = (f32[32,1,160]{2,1,0:T(1,128)S(1)}, f32[32,1,160]{2,1,0:T(1,128)S(1)}, u32[]{:S(2)}, u32[]{:S(2)}) collective-permute-start(f32[32,1,160]{2,1,0:T(1,128)S(1)} %fusion.80), channel_id=1, source_target_pairs={{0,4},{4,8},{8,12},{12,16},{16,20},{20,24},{24,28},{1,5},{5,9},{9,... | collective-permute-start | bytes 61448 | tf_op jit(solution)/shard_map/ppermute | solution.py:20
Sparse Core Ops, SparseCore 0:
  87.5 133.4 all-reduce.3
where the time goes:
time: 240 us; the launch traced here: 239 us
  waiting for transfers between devices  94.6 us (39%)
  blocking collectives  41.9 us (17%)
  matrix products  31.7 us (13%)
  starting transfers between devices  21.1 us (9%)
  between operations  19.8 us (8%)
  other arithmetic  17.7 us (7%)
  local copies, waits for them, and re-layouts  12.2 us (5%)
    psum x1, waiting for transfers between devices, shards(): lax.psum((grad_in, grad_mid, grad_out), ('row', 'col'))  86.2 us
    psum x1, blocking collectives, grid_total_sum(): return lax.psum(grid_local, ('row', 'col'))  41.9 us
    ppermute x8, starting transfers between devices, shifted(): return lax.ppermute(block, axis, route)  21.1 us
    dot_general x3, matrix products, contract_cols(): lax.dot_general(former, latter, (((1,), (1,)), ((), ())), preferred_eleme...  9.93 us
    div x5, other arithmetic, adam_step(): new_one / (1.0 - BETA_ONE ** ADAM_STEP)  9.62 us
    dot_general x3, matrix products, contract_rows(): lax.dot_general(former, latter, (((0,), (0,)), ((), ())), preferred_eleme...  8.45 us
    ppermute x8, waiting for transfers between devices, shifted(): return lax.ppermute(block, axis, route)  8.35 us
    dot_general x3, matrix products, matmul(): return jnp.dot(former, latter, preferred_element_type=jnp.float32)  6.85 us
  transfers between devices with their start and end apart: 9, of which 6 were waited for; matrix products, arithmetic and copies ran while one was open for 7% of the time, Pallas kernels for 0%

commit v1 on v0

--- a/solution.py
+++ b/solution.py
@@ -143,7 +143,7 @@
 
 
 def grid_total_sum(grid_local):
-    return lax.psum(grid_local, ("row", "col"))
+    return jnp.sum(lax.all_gather(grid_local, ("row", "col")), axis=0)
 
 
 def shards(

time: 240 us -> 248 us (1.033)
  matrix products: 31.7 us -> 36 us
    psum x1 -> x0, blocking collectives: 41.9 us -> none  [grid_total_sum(): return lax.psum(grid_local, ('row', 'col'))]
    unnamed x0 -> x1, blocking collectives: none -> 40.5 us
    unnamed x32 -> x36, local copies, waits for them, and re-layouts: 4.27 us -> 8.19 us
  transfers between devices with their start and end apart: 9 -> 9, of which waited for: 6 -> 6; matrix products, arithmetic and copies ran while one was open for 7% -> 6% of each run, Pallas kernels for 0% -> 0%
where the time goes in v1:
time: 248 us; the launch traced here: 247 us
  waiting for transfers between devices  95.6 us (39%)
  blocking collectives  40.5 us (16%)
  matrix products  36 us (15%)
  starting transfers between devices  21.5 us (9%)
  between operations  19.8 us (8%)
  other arithmetic  19 us (8%)
  local copies, waits for them, and re-layouts  14.6 us (6%)
    psum x1, waiting for transfers between devices, shards(): lax.psum((grad_in, grad_mid, grad_out), ('row', 'col'))  86 us
    unnamed x1, blocking collectives  40.5 us
    ppermute x8, starting transfers between devices, shifted(): return lax.ppermute(block, axis, route)  21.5 us
    dot_general x3, matrix products, contract_rows(): lax.dot_general(former, latter, (((0,), (0,)), ((), ())), preferred_eleme...  10.7 us
    dot_general x3, matrix products, contract_cols(): lax.dot_general(former, latter, (((1,), (1,)), ((), ())), preferred_eleme...  9.94 us
    div x5, other arithmetic, adam_step(): new_one / (1.0 - BETA_ONE ** ADAM_STEP)  9.71 us
    ppermute x8, waiting for transfers between devices, shifted(): return lax.ppermute(block, axis, route)  9.59 us
    dot_general x3, matrix products, matmul(): return jnp.dot(former, latter, preferred_element_type=jnp.float32)  8.91 us
  transfers between devices with their start and end apart: 9, of which 6 were waited for; matrix products, arithmetic and copies ran while one was open for 6% of the time, Pallas kernels for 0%

profile of v1, /device:TPU:0, one launch (start us, length us, event | category | flops | bytes accessed | tf_op | source)
XLA Modules:
  0.0 247.0 jit_solution(14858821211089982279)
XLA Ops:
  7.2 1.0 copy.59
  8.2 0.9 slice.117
  9.2 1.3 collective-permute-start
  10.5 1.3 fusion.148
  13.2 0.9 slice_bitcast_fusion.2
  14.1 1.9 collective-permute-done
  16.3 1.1 pad_maximum_fusion
  17.8 1.3 collective-permute-start.1
  19.1 1.8 collective-permute-done.1
  21.6 2.2 fusion.14
  23.8 0.6 convolution_convert_fusion.1
  24.9 0.6 convolution_convert_fusion
  25.6 1.3 fusion.82
  26.9 6.5 %fusion.5 = (bf16[512,4096]{0,1:T(8,128)(2,1)S(1)}, f32[4096,512]{1,0:T(8,128)}) fusion(f32[1,512,512]{2,1,0:T(8,128)S(1)} %copy-done.10, f32[4096,512]{1,0:T(8,128)S(1)} %fusion.82), kind=kOutput, calls=%fused_computation.10 | convolution fusion | flops 2168717312 | bytes 22020096 | tf_op jit(solution)/shard_map/dot_general | solution.py:80
  33.4 1.9 copy-done
  35.4 1.2 fusion.125
  36.6 1.3 collective-permute-start.4
  37.9 1.3 collective-permute-start.2
  39.3 2.3 collective-permute-done.4
  41.6 2.6 %collective-permute-done.2 = f32[3,1,128]{2,1,0:T(1,128)S(1)} collective-permute-done((f32[3,1,128]{2,1,0:T(1,128)S(1)}, f32[3,1,128]{2,1,0:T(1,128)S(1)}, u32[]{:S(2)}, u32[]{:S(2)}) %collective-permute-start.2) | collective-permute-done | bytes 1568 | tf_op jit(solution)/shard_map/ppermute | solution.py:20
  44.4 3.5 %collective-permute-start.5 = (f32[3,32,1]{2,1,0:T(8,128)S(1)}, f32[3,32,1]{2,1,0:T(8,128)S(1)}, u32[]{:S(2)}, u32[]{:S(2)}) collective-permute-start(f32[3,32,1]{2,1,0:T(8,128)S(1)} %slice.167), channel_id=1, source_target_pairs={{0,1},{1,2},{2,3},{4,5},{5,6},{6,7},{8,9},{9,10},{10,11},{12,13},{... | collective-permute-start | bytes 1160 | tf_op jit(solution)/shard_map/ppermute | solution.py:20
  48.0 4.7 %collective-permute-start.3 = (f32[3,1,128]{2,1,0:T(1,128)S(1)}, f32[3,1,128]{2,1,0:T(1,128)S(1)}, u32[]{:S(2)}, u32[]{:S(2)}) collective-permute-start(f32[3,1,128]{2,1,0:T(1,128)S(1)} %slice.163), channel_id=1, source_target_pairs={{0,4},{4,8},{8,12},{12,16},{16,20},{20,24},{24,28},{1,5},{5,9},{9,... | collective-permute-start | bytes 4616 | tf_op jit(solution)/shard_map/ppermute | solution.py:20
  52.8 1.0 collective-permute-done.3
  54.1 5.8 %fusion.1 = bf16[512,4096]{0,1:T(8,128)(2,1)S(1)} fusion(f32[4096,512]{1,0:T(8,128)} %get-tuple-element.27, bf16[3,4096]{1,0:T(4,128)(2,1)S(1)} %fusion.63, f32[3,512]{1,0:T(4,128)S(1)} %copy-done.7), kind=kOutput, calls=%fused_computation.3 | convolution fusion | flops 31458816 | bytes 12613632 | tf_op jit(solution)/shard_map/dot_general | solution.py:84
  59.9 3.4 %convolution_bitcast_fusion.1 = f32[1,512,512]{2,1,0:T(8,128)} fusion(bf16[512,4096]{0,1:T(8,128)(2,1)S(1)} %fusion.1, f32[4096,512]{1,0:T(8,128)S(1)} %bitcast.208), kind=kOutput, calls=%fused_computation.24 | convolution fusion | flops 2157969408 | bytes 13631488 | tf_op jit(solution)/shard_map/dot_general | solution.py:90
  63.3 3.6 %fusion = bf16[512,4096]{0,1:T(8,128)(2,1)S(1)} fusion(f32[4096,512]{1,0:T(8,128)S(1)} %bitcast.208, bf16[512,4096]{0,1:T(8,128)(2,1)S(1)} %fusion.1, f32[1,512,512]{2,1,0:T(8,128)S(1)} %copy-done.10), kind=kOutput, calls=%fused_computation.1 | convolution fusion | flops 2166620160 | bytes 17825792 | tf_op jit(solution)/shard_map/dot_general | solution.py:84
  66.9 1.9 copy-done.1
  68.9 1.4 convolution_bitcast_fusion
  70.3 0.9 slice_bitcast_fusion
  71.2 0.8 convolution_bitcast_fusion.2
  72.0 1.2 fusion.56
  73.6 1.1 copy.92
  76.0 3.9 %collective-permute-start.6 = (f32[32,42,1]{1,0,2:T(8,128)S(1)}, f32[32,42,1]{1,0,2:T(8,128)S(1)}, u32[]{:S(2)}, u32[]{:S(2)}) collective-permute-start(f32[32,42,1]{1,0,2:T(8,128)S(1)} %pad_maximum_fusion.8), channel_id=1, source_target_pairs={{0,1},{1,2},{2,3},{4,5},{5,6},{6,7},{8,9},{9,10},{10,11},{12,13},{... | collective-permute-start | bytes 16136 | tf_op jit(solution)/shard_map/ppermute | solution.py:20
  79.9 3.7 %fusion.150 = f32[512,64]{0,1:T(8,128)} fusion(bf16[64,4096]{1,0:T(8,128)(2,1)S(1)} %bitcast_dynamic-update-slice_fusion, bf16[512,4096]{0,1:T(8,128)(2,1)} %copy-done.1), kind=kOutput, calls=%fused_computation.235 | convolution fusion | flops 268435456 | bytes 4849664 | tf_op jit(solution)/shard_map/dot_general | solution.py:90
  85.6 4.1 %collective-permute-start.7 = (f32[32,1,160]{2,1,0:T(1,128)S(1)}, f32[32,1,160]{2,1,0:T(1,128)S(1)}, u32[]{:S(2)}, u32[]{:S(2)}) collective-permute-start(f32[32,1,160]{2,1,0:T(1,128)S(1)} %fusion.80), channel_id=1, source_target_pairs={{0,4},{4,8},{8,12},{12,16},{16,20},{20,24},{24,28},{1,5},{5,9},{9,... | collective-permute-start | bytes 61448 | tf_op jit(solution)/shard_map/ppermute | solution.py:20
  89.7 2.8 %fusion.149 = f32[3,512]{1,0:T(4,128)S(1)} fusion(bf16[3,4096]{1,0:T(4,128)(2,1)S(1)} %fusion.63, bf16[512,4096]{0,1:T(8,128)(2,1)} %copy-done), kind=kOutput, calls=%fused_computation.234 | convolution fusion | flops 12582912 | bytes 4225024 | tf_op jit(solution)/shard_map/dot_general | solution.py:90
  92.6 1.4 multiply_reduce_fusion.3
  94.1 0.8 multiply_reduce_fusion.1
  96.4 40.5 %all-reduce.1 = (f32[32]{0:T(128)S(1)}, f32[3,512]{1,0:T(4,128)S(1)}) all-reduce(f32[32]{0:T(128)S(1)} %dynamic-update-slice, f32[3,512]{1,0:T(4,128)S(1)} %fusion.149), channel_id=1, replica_groups=mesh['row'=8,'col'=4] {'row','col'}, use_global_device_ids=true, to_apply=%add | all-reduce | flops 1568 | bytes 12544
  138.2 0.7 multiply_reduce_fusion.4
  138.9 1.8 fusion.49
  140.7 2.3 fusion.29
  143.0 86.0 %all-reduce.5.cloned.1.call-done = (f32[512,64]{0,1:T(8,128)}, f32[1,512,512]{2,1,0:T(8,128)}) async-done(((f32[512,64]{0,1:T(8,128)}, f32[1,512,512]{2,1,0:T(8,128)}), (f32[512,64]{0,1:T(8,128)}, f32[1,512,512]{2,1,0:T(8,128)})) %all-reduce.5.cloned.1.call-update) | async-done | bytes 1179664 | tf_op jit(solution)/shard_map/psum | solution.py:250
  229.0 2.1 multiply_reduce_fusion
  231.1 1.5 multiply_reduce_fusion.2
  234.6 0.6 fusion.103
  235.2 3.2 %fusion.24 = f32[1,512,512]{2,1,0:T(8,128)} fusion(f32[1,512,512]{2,1,0:T(8,128)S(1)} %copy-done.3, f32[1,512,512]{2,1,0:T(8,128)} %get-tuple-element.8, f32[1,512,512]{2,1,0:T(8,128)} %param.30, f32[]{:T(128)S(6)} %min.7), kind=kLoop, calls=%fused_computation.39 | loop fusion | flops 3145728 | bytes 4194308 | tf_op jit(solution)/shard_map/div | solution.py:139
  238.4 1.8 fusion.54
  (87 shorter events, 7.4 us)
Async XLA Ops:
  7.2 18.4 %copy-start.4 = (f32[512,64]{0,1:T(8,128)S(1)}, f32[512,64]{0,1:T(8,128)}, u32[]{:S(2)}) copy-start(f32[512,64]{0,1:T(8,128)} %param.21) | copy-start | bytes 393220
  7.2 221.8 %all-reduce.5.cloned.1.call-start = ((), (), s32[]{:S(2)}) async-start(), calls=%async_computation | async-start | bytes 2359296 | tf_op jit(solution)/shard_map/psum | solution.py:250
  9.2 6.8 %collective-permute-start = (f32[32,1,160]{2,1,0:T(1,128)S(1)}, f32[32,1,160]{2,1,0:T(1,128)S(1)}, u32[]{:S(2)}, u32[]{:S(2)}) collective-permute-start(f32[32,1,160]{2,1,0:T(1,128)S(1)} %copy.60), channel_id=1, source_target_pairs={{4,0},{8,4},{12,8},{16,12},{20,16},{24,20},{28,24},{5,1},{9,5},{13... | collective-permute-start | bytes 61448 | tf_op jit(solution)/shard_map/ppermute | solution.py:20
  17.8 3.1 %collective-permute-start.1 = (f32[32,42,1]{1,0,2:T(8,128)S(1)}, f32[32,42,1]{1,0,2:T(8,128)S(1)}, u32[]{:S(2)}, u32[]{:S(2)}) collective-permute-start(f32[32,42,1]{1,0,2:T(8,128)S(1)} %pad_maximum_fusion.7), channel_id=1, source_target_pairs={{1,0},{2,1},{3,2},{5,4},{6,5},{7,6},{9,8},{10,9},{11,10},{13,12},{... | collective-permute-start | bytes 16136 | tf_op jit(solution)/shard_map/ppermute | solution.py:20
  23.8 3.1 %copy-start.10 = (f32[1,512,512]{2,1,0:T(8,128)S(1)}, f32[1,512,512]{2,1,0:T(8,128)}, u32[]{:S(2)}) copy-start(f32[1,512,512]{2,1,0:T(8,128)} %param.22) | copy-start | bytes 3145732
  26.9 6.5 %copy-start.2 = (f32[4096,512]{1,0:T(8,128)}, f32[4096,512]{1,0:T(8,128)S(1)}, u32[]{:S(2)}) copy-start(f32[4096,512]{1,0:T(8,128)S(1)} %fusion.82) | copy-start | bytes 25165828
  26.9 8.4 %copy-start.7 = (f32[3,512]{1,0:T(4,128)S(1)}, f32[3,512]{1,0:T(4,128)}, u32[]{:S(2)}) copy-start(f32[3,512]{1,0:T(4,128)} %param.23) | copy-start | bytes 18436
  26.9 17.3 %copy-start.6 = (f32[3,3,32,128]{3,2,1,0:T(8,128)S(1)}, f32[3,3,32,128]{3,2,1,0:T(8,128)}, u32[]{:S(2)}) copy-start(f32[3,3,32,128]{3,2,1,0:T(8,128)} %param.18) | copy-start | bytes 442372
  33.4 2.0 copy-start
  36.6 5.0 %collective-permute-start.4 = (f32[3,32,1]{2,1,0:T(8,128)S(1)}, f32[3,32,1]{2,1,0:T(8,128)S(1)}, u32[]{:S(2)}, u32[]{:S(2)}) collective-permute-start(f32[3,32,1]{2,1,0:T(8,128)S(1)} %bitcast.216), channel_id=1, source_target_pairs={{1,0},{2,1},{3,2},{5,4},{6,5},{7,6},{9,8},{10,9},{11,10},{13,12},{... | collective-permute-start | bytes 1160 | tf_op jit(solution)/shard_map/ppermute | solution.py:20
  37.9 6.4 %collective-permute-start.2 = (f32[3,1,128]{2,1,0:T(1,128)S(1)}, f32[3,1,128]{2,1,0:T(1,128)S(1)}, u32[]{:S(2)}, u32[]{:S(2)}) collective-permute-start(f32[3,1,128]{2,1,0:T(1,128)S(1)} %slice.162), channel_id=1, source_target_pairs={{4,0},{8,4},{12,8},{16,12},{20,16},{24,20},{28,24},{5,1},{9,5},{13... | collective-permute-start | bytes 4616 | tf_op jit(solution)/shard_map/ppermute | solution.py:20
  44.4 8.3 %collective-permute-start.5 = (f32[3,32,1]{2,1,0:T(8,128)S(1)}, f32[3,32,1]{2,1,0:T(8,128)S(1)}, u32[]{:S(2)}, u32[]{:S(2)}) collective-permute-start(f32[3,32,1]{2,1,0:T(8,128)S(1)} %slice.167), channel_id=1, source_target_pairs={{0,1},{1,2},{2,3},{4,5},{5,6},{6,7},{8,9},{9,10},{10,11},{12,13},{... | collective-permute-start | bytes 1160 | tf_op jit(solution)/shard_map/ppermute | solution.py:20
  48.0 5.8 %collective-permute-start.3 = (f32[3,1,128]{2,1,0:T(1,128)S(1)}, f32[3,1,128]{2,1,0:T(1,128)S(1)}, u32[]{:S(2)}, u32[]{:S(2)}) collective-permute-start(f32[3,1,128]{2,1,0:T(1,128)S(1)} %slice.163), channel_id=1, source_target_pairs={{0,4},{4,8},{8,12},{12,16},{16,20},{20,24},{24,28},{1,5},{5,9},{9,... | collective-permute-start | bytes 4616 | tf_op jit(solution)/shard_map/ppermute | solution.py:20
  53.8 6.1 %slice-start = ((s8[8388608]{0:T(1024)(128)(4,1)}), s8[4194304]{0:T(1024)(128)(4,1)S(1)}, s32[]{:S(2)}) async-start(s8[8388608]{0:T(1024)(128)(4,1)} %bitcast.207), calls=%async_computation.1 | async-start | bytes 8388608
  54.1 5.8 %slice-start.1 = ((s8[8388608]{0:T(1024)(128)(4,1)}), s8[4194304]{0:T(1024)(128)(4,1)S(1)}, s32[]{:S(2)}) async-start(s8[8388608]{0:T(1024)(128)(4,1)} %bitcast.207), calls=%async_computation.2 | async-start | bytes 8388608
  66.9 2.0 copy-start.1
  76.0 8.7 %collective-permute-start.6 = (f32[32,42,1]{1,0,2:T(8,128)S(1)}, f32[32,42,1]{1,0,2:T(8,128)S(1)}, u32[]{:S(2)}, u32[]{:S(2)}) collective-permute-start(f32[32,42,1]{1,0,2:T(8,128)S(1)} %pad_maximum_fusion.8), channel_id=1, source_target_pairs={{0,1},{1,2},{2,3},{4,5},{5,6},{6,7},{8,9},{9,10},{10,11},{12,13},{... | collective-permute-start | bytes 16136 | tf_op jit(solution)/shard_map/ppermute | solution.py:20
  83.6 57.1 %copy-start.5 = (f32[32,32,128]{2,1,0:T(8,128)S(1)}, f32[32,32,128]{2,1,0:T(8,128)}, u32[]{:S(2)}) copy-start(f32[32,32,128]{2,1,0:T(8,128)} %param.25) | copy-start | bytes 1572868
  84.7 149.8 %copy-start.8 = (f32[3,512]{1,0:T(4,128)S(1)}, f32[3,512]{1,0:T(4,128)}, u32[]{:S(2)}) copy-start(f32[3,512]{1,0:T(4,128)} %param.33) | copy-start | bytes 18436
  84.7 149.9 %copy-start.9 = (f32[3,512]{1,0:T(4,128)S(1)}, f32[3,512]{1,0:T(4,128)}, u32[]{:S(2)}) copy-start(f32[3,512]{1,0:T(4,128)} %param.32) | copy-start | bytes 18436
  84.7 150.5 %copy-start.3 = (f32[1,512,512]{2,1,0:T(8,128)S(1)}, f32[1,512,512]{2,1,0:T(8,128)}, u32[]{:S(2)}) copy-start(f32[1,512,512]{2,1,0:T(8,128)} %param.31) | copy-start | bytes 3145732
  85.6 6.9 %collective-permute-start.7 = (f32[32,1,160]{2,1,0:T(1,128)S(1)}, f32[32,1,160]{2,1,0:T(1,128)S(1)}, u32[]{:S(2)}, u32[]{:S(2)}) collective-permute-start(f32[32,1,160]{2,1,0:T(1,128)S(1)} %fusion.80), channel_id=1, source_target_pairs={{0,4},{4,8},{8,12},{12,16},{16,20},{20,24},{24,28},{1,5},{5,9},{9,... | collective-permute-start | bytes 61448 | tf_op jit(solution)/shard_map/ppermute | solution.py:20
Sparse Core Ops, SparseCore 0:
  96.5 132.4 all-reduce.4
